TPU v7x, 256 devices: a whole 4x4x8 slice. The times are simulated.
256 devices in a mesh: seq: 8 (over y, x_lo), blk: 32 (over z, x_hi, core).
Axes of the slice: x: 4 (x_hi: 2, x_lo: 2; x = x_hi * 2 + x_lo), y: 4, z: 8, core: 2. Of those that a mesh axis runs over, the one named last changes fastest.
Arguments:
- activations: bfloat16 [2, 64, 1024, 4096], P(None, 'blk', 'seq'), may hold values from -120 to 120, as said below
- out_grads: bfloat16 [2, 64, 1024, 4096], P(None, 'blk', 'seq'), may hold values from -120 to 120, as said below
- lengths: int32 [64], P('blk'), may hold values from 512 to 1024
- input_proj: bfloat16 [2, 64, 4096], replicated, may hold values from -0.09375 to 0.09375
- output_proj: bfloat16 [2, 64, 4096], replicated, may hold values from -0.09375 to 0.09375
- stored_proj: float32 [16384, 2, 64, 64], P(('seq', 'blk')), may hold values from -6 to 6
Outputs:
- scores: float32 [64, 16384], P('blk', 'seq')
Inputs may be any that keep to these rules, and one draw needn't show every extreme that they name: `activations`: finite values. `out_grads`: finite values.
All inputs are finite; a program needn't handle non-finite values.
Results may differ from a plain program's by a relative error of at most 0.0003.
Values sent between devices are 32-bit elements; how exact they have to be, the bound alone decides.
No kernel may reach another device: no remote copies, remote signals or barrier semaphores. Data moves between devices by JAX's collectives and lax.ppermute only.
A program may use at most 64 MiB of HBM per device.

v0:
```python
import math
import jax
import jax.numpy as jnp
from jax import lax
from jax.sharding import PartitionSpec as P

damping = 0.1


def cut_along(x, dim, devices):
    before, after = (x.shape[:dim], x.shape[dim + 1 :])
    return jnp.moveaxis(x.reshape(*before, devices, -1, *after), dim, 0)


def sum_at_owner(x, axis, dim):
    pieces = cut_along(x, dim, lax.axis_size(axis))
    arrived = lax.all_to_all(pieces, axis, split_axis=0, concat_axis=0, tiled=True)
    return arrived.sum(axis=0)


def sent_together(arrays, axis, dim, along):
    columns = [a.reshape(*a.shape[:along], -1) for a in arrays]
    both = jnp.concatenate(columns, axis=along)
    whole, at, finished = (sum_at_owner(both, axis, dim), 0, [])
    for a, column in zip(arrays, columns):
        section = whole[..., at : at + column.shape[along]]
        finished.append(section.reshape(*section.shape[:along], *a.shape[along:]))
        at += column.shape[along]
    return tuple(finished)


def sent_to_all(x, axis):
    copies = jnp.broadcast_to(x, (lax.axis_size(axis), *x.shape))
    return lax.all_to_all(copies, axis, split_axis=0, concat_axis=0, tiled=True)


def of_everyone(x, axis):
    return sent_to_all(x, axis).sum(axis=0)


def together(arrays, axis):
    ravelled, at, finished = (jnp.concatenate([a.reshape(-1) for a in arrays]), 0, [])
    so_far = of_everyone(ravelled, axis)
    for a in arrays:
        finished.append(so_far[at : at + a.size].reshape(a.shape))
        at += a.size
    return tuple(finished)


def sent_together_2(arrays, axis, dim, along):
    widths = [a.shape[along] for a in arrays]
    both = jnp.concatenate(arrays, axis=along)
    whole = lax.all_gather(both, axis, axis=dim, tiled=True)
    return tuple(jnp.split(whole, [sum(widths[:k]) for k in range(1, len(widths))], axis=along))


def in_order(pieces, dim):
    shape = list(pieces.shape[1:])
    shape[dim] *= pieces.shape[0]
    return jnp.moveaxis(pieces, 0, dim).reshape(shape)


def gathered_copies(x, axis, dim):
    pieces = sent_to_all(x, axis)
    return in_order(pieces, dim)


def damped_inverse(moment, token_count):
    moment_mean = jnp.transpose(moment, (1, 0, 2)) / token_count
    proj_rank = moment_mean.shape[-1]
    identity = jnp.eye(proj_rank, dtype=jnp.float32)
    trace_part = jnp.trace(moment_mean, axis1=1, axis2=2)
    damped = moment_mean + (damping * trace_part / proj_rank)[:, None, None] * identity
    factor_low = jnp.linalg.cholesky(damped)
    return jax.vmap(lambda lower: jax.scipy.linalg.cho_solve((lower, True), identity))(factor_low)


def shards(activations, out_grads, lengths, input_proj, output_proj, stored_proj):
    hp = lax.Precision.HIGHEST
    layers, roll_dev, seq_dev, model_width = activations.shape
    proj_rank = input_proj.shape[1]
    seq_index = lax.axis_index("seq")
    blk_count = lax.axis_size("blk")
    train_dev = stored_proj.shape[0]
    positions = seq_index * seq_dev + jnp.arange(seq_dev, dtype=jnp.int32)
    live_mask = (positions[None, :] < lengths[:, None]).astype(jnp.float32)
    projected_in = (
        jnp.einsum("lrsd,lkd->lrsk", activations, input_proj, preferred_element_type=jnp.float32)
        * live_mask[None, :, :, None]
    )
    projected_out = (
        jnp.einsum("lrsd,lkd->lrsk", out_grads, output_proj, preferred_element_type=jnp.float32)
        * live_mask[None, :, :, None]
    )
    moment_in = jnp.einsum("lrsk,lrsm->klm", projected_in, projected_in, precision=hp)
    moment_out = jnp.einsum("lrsk,lrsm->klm", projected_out, projected_out, precision=hp)
    grad_terms = jnp.einsum("lrsp,lrsq->prlq", projected_out, projected_in, precision=hp)
    grad_rows, in_rows, out_rows = sent_together((grad_terms, moment_in, moment_out), "seq", 0, 2)
    local_count = jnp.sum(lengths).astype(jnp.float32)
    in_rows, out_rows, token_count = together((in_rows, out_rows, local_count), "blk")
    moment_in, moment_out = sent_together_2((in_rows, out_rows), "seq", 0, 1)
    factor_in = damped_inverse(moment_in, token_count)
    factor_out = damped_inverse(moment_out, token_count)
    right_done = jnp.einsum("prlq,lqk->prlk", grad_rows, factor_in, precision=hp)
    precond = jnp.zeros((proj_rank, roll_dev, layers, proj_rank), jnp.float32) + jnp.einsum(
        "lap,prlk->arlk", factor_out, gathered_copies(right_done, "seq", 0), precision=hp
    )
    norm_scale = 1.0 / math.sqrt(layers * proj_rank * proj_rank)
    empty_scores = jnp.zeros((roll_dev * blk_count, train_dev), jnp.float32)
    partial_scores = (
        jnp.einsum("prlk,tlpk->rt", gathered_copies(precond, "blk", 1), stored_proj, precision=hp)
        * norm_scale
    )
    local_scores = lax.dynamic_update_slice_in_dim(empty_scores, partial_scores, jnp.int32(0), 0)
    return lax.all_to_all(local_scores, "blk", split_axis=0, concat_axis=1, tiled=True)


def solution(mesh):
    return jax.shard_map(
        shards,
        mesh=mesh,
        in_specs=(
            P(None, "blk", "seq", None),
            P(None, "blk", "seq", None),
            P("blk"),
            P(),
            P(),
            P(("seq", "blk"), None, None, None),
        ),
        out_specs=P("blk", "seq"),
        check_vma=False,
    )
```

profile of v0, /device:TPU:1, one launch (start us, length us, event | category | flops | bytes accessed | tf_op | source)
XLA Modules:
  0.0 239.5 jit_solution(14124205600926753591)
XLA Ops:
  0.0 0.9 compare_convert_fusion
  0.9 0.3 copy-done
  1.2 4.1 %convolution_multiply_fusion = f32[2,2,128,64]{2,3,1,0:T(8,128)S(1)} fusion(bf16[2,2,128,4096]{3,2,1,0:T(8,128)(2,1)} %param.10, bf16[2,64,4096]{2,1,0:T(8,128)(2,1)S(1)} %copy-done, f32[2,128]{1,0:T(2,128)S(1)} %compare_convert_fusion), kind=kOutput, calls=%fused_computation.2 | convolution fusion | flops 268468224 | bytes 5374976 | tf_op jit(solution)/shard_map/lrsd,lkd->lrsk/dot_general | solution.py:92
  5.4 0.3 convolution_bitcast_fusion.4
  5.7 1.4 convolution_multiply_fusion.1
  7.1 0.3 convolution_bitcast_fusion.1
  7.4 0.3 convolution_bitcast_fusion.5
  7.9 0.1 copy.108
  8.0 0.1 concatenate.16
  8.1 0.1 pad_maximum_fusion
  8.2 0.6 copy.111
  8.8 5.9 %all-to-all-start = ((f32[8,8,2,256]{3,1,2,0:T(8,128)}), f32[8,8,2,256]{3,1,2,0:T(8,128)S(1)}, u32[]{:S(2)}, u32[]{:S(2)}) async-start(f32[8,8,2,256]{3,1,2,0:T(8,128)} %copy.111), calls=%async_computation | async-start | bytes 262144 | tf_op jit(solution)/shard_map/all_to_all | solution.py:17
  14.8 0.6 reduce_sum.44
  16.1 4.3 %all-to-all-done = f32[8,8,2,256]{3,1,2,0:T(8,128)S(1)} async-done(((f32[8,8,2,256]{3,1,2,0:T(8,128)}), f32[8,8,2,256]{3,1,2,0:T(8,128)S(1)}, u32[]{:S(2)}, u32[]{:S(2)}) %all-to-all-start) | async-done | bytes 131104 | tf_op jit(solution)/shard_map/all_to_all | solution.py:17
  20.4 0.1 reshape.100
  20.5 0.1 reshape.101
  20.6 0.8 broadcast_in_dim.37
  21.5 12.9 %all-to-all-start.1 = ((f32[32,1,2049]{2,1,0:T(1,128)}), f32[32,1,2049]{2,1,0:T(1,128)S(1)}, u32[]{:S(2)}, u32[]{:S(2)}) async-start(f32[32,1,2049]{2,1,0:T(1,128)} %broadcast_in_dim.37), calls=%async_computation.1 | async-start | bytes 557056 | tf_op jit(solution)/shard_map/all_to_all | solution.py:34
  34.5 0.1 reshape.106
  34.6 13.0 %all-to-all-done.1 = f32[32,1,2049]{2,1,0:T(1,128)S(1)} async-done(((f32[32,1,2049]{2,1,0:T(1,128)}), f32[32,1,2049]{2,1,0:T(1,128)S(1)}, u32[]{:S(2)}, u32[]{:S(2)}) %all-to-all-start.1) | async-done | bytes 262304 | tf_op jit(solution)/shard_map/all_to_all | solution.py:34
  47.6 0.2 reduce_sum.45
  47.7 0.5 slice.40
  48.2 0.1 reshape.103
  48.4 21.9 %all_gather.3 = f32[64,4,64]{2,1,0:T(4,128)S(1)} all-gather(f32[8,4,64]{2,1,0:T(4,128)S(1)} %pad_maximum_fusion.1), channel_id=1, replica_groups=mesh['seq'=8,'blk'=32] {'seq'}, dimensions={0}, use_global_device_ids=true | all-gather | bytes 73728 | tf_op jit(solution)/shard_map/all_gather | solution.py:53
  70.4 0.1 copy.147
  70.5 0.1 copy.145
  70.6 0.8 fusion.15
  71.4 0.7 bitcast_add_fusion.3
  72.2 11.7 %custom-call.10 = f32[2,64,64]{2,1,0:T(8,128)S(1)} custom-call(f32[2,64,64]{2,1,0:T(8,128)S(1)} %fusion.14), custom_call_target="Cholesky" | custom-call | tf_op jit(solution)/shard_map/jit(cholesky)/cholesky | solution.py:74
  83.9 0.1 copy.123
  84.0 11.7 %custom-call.12 = f32[2,64,64]{2,1,0:T(8,128)S(1)} custom-call(f32[2,64,64]{2,1,0:T(8,128)S(1)} %fusion.9), custom_call_target="Cholesky" | custom-call | tf_op jit(solution)/shard_map/jit(cholesky)/cholesky | solution.py:74
  95.8 0.1 compare_reduce_fusion.1
  95.9 0.1 compare_reduce_fusion
  96.1 0.1 select_bitcast_fusion.1
  96.2 9.8 %custom-call.11 = f32[2,1,64,64]{2,3,1,0:T(8,128)S(1)} custom-call(f32[2,1,64,64]{3,2,1,0:T(8,128)S(1)} %get-tuple-element.19), custom_call_target="InvertDiagBlocksLowerTriangular" | custom-call | tf_op jit(solution)/shard_map/vmap(jit(_cho_solve))/triangular_solve | solution.py:75
  106.0 9.8 %custom-call.13 = f32[2,1,64,64]{2,3,1,0:T(8,128)S(1)} custom-call(f32[2,1,64,64]{3,2,1,0:T(8,128)S(1)} %get-tuple-element.20), custom_call_target="InvertDiagBlocksLowerTriangular" | custom-call | tf_op jit(solution)/shard_map/vmap(jit(_cho_solve))/triangular_solve | solution.py:75
  115.8 0.3 fusion.7
  116.1 0.3 fusion.12
  116.4 0.2 convolution_bitcast_fusion.3
  116.6 0.2 convolution_bitcast_fusion.7
  116.8 0.7 reshape.116
  117.6 3.5 %all-to-all-start.2 = ((f32[8,1,2048]{2,1,0:T(1,128)}), f32[8,1,2048]{2,1,0:T(1,128)S(1)}, u32[]{:S(2)}, u32[]{:S(2)}) async-start(f32[8,1,2048]{2,1,0:T(1,128)} %reshape.116), calls=%async_computation.2 | async-start | bytes 131072 | tf_op jit(solution)/shard_map/all_to_all | solution.py:34
  121.1 0.2 convolution_bitcast_fusion.2
  121.3 4.7 %all-to-all-done.2 = f32[8,1,2048]{2,1,0:T(1,128)S(1)} async-done(((f32[8,1,2048]{2,1,0:T(1,128)}), f32[8,1,2048]{2,1,0:T(1,128)S(1)}, u32[]{:S(2)}, u32[]{:S(2)}) %all-to-all-start.2) | async-done | bytes 65568 | tf_op jit(solution)/shard_map/all_to_all | solution.py:34
  126.1 0.5 broadcast.96
  126.6 0.8 reduce.5
  127.4 0.1 reshape.117
  127.5 0.4 convolution_bitcast_fusion
  127.8 0.1 copy.127
  128.0 3.8 %broadcast_bitcast_fusion = f32[32,64,2,2,64]{4,3,2,1,0:T(2,128)} fusion(f32[64,2,2,64]{0,1,2,3:T(2,128)S(1)} %copy.127), kind=kLoop, calls=%fused_computation.59 | loop fusion | bytes 2162688
  131.8 6.6 %reshape.118 = f32[32,1,16384]{2,1,0:T(1,128)} reshape(f32[32,64,2,2,64]{4,3,2,1,0:T(2,128)} %broadcast_bitcast_fusion) | data formatting | bytes 4194304
  138.4 12.3 %all-to-all-start.3 = ((f32[32,1,16384]{2,1,0:T(1,128)}), f32[32,1,16384]{2,1,0:T(1,128)}, u32[]{:S(2)}, u32[]{:S(2)}) async-start(f32[32,1,16384]{2,1,0:T(1,128)} %reshape.118), calls=%async_computation.3 | async-start | bytes 4194304 | tf_op jit(solution)/shard_map/all_to_all | solution.py:34
  150.6 5.7 %copy.129 = f32[64,2,64,64]{2,0,1,3:T(8,128)} copy(f32[64,2,64,64]{3,2,1,0:T(8,128)} %param.14) | data formatting | bytes 4194304 | tf_op args[5]
  156.3 44.4 %all-to-all-done.3 = f32[32,1,16384]{2,1,0:T(1,128)} async-done(((f32[32,1,16384]{2,1,0:T(1,128)}), f32[32,1,16384]{2,1,0:T(1,128)}, u32[]{:S(2)}, u32[]{:S(2)}) %all-to-all-start.3) | async-done | bytes 2097184 | tf_op jit(solution)/shard_map/all_to_all | solution.py:34
  200.7 7.4 %reduce.6 = f32[32,16384]{1,0:T(8,128)S(1)} reduce(f32[32,1,16384]{2,1,0:T(1,128)} %all-to-all-done.3, f32[]{:T(128)} %broadcast.96), dimensions={1}, to_apply=%all_to_all.30.reduce_sub_computation | reduce | bytes 4194308 | tf_op jit(solution)/shard_map/all_to_all | solution.py:34
  208.1 4.4 %reshape.119 = f32[32,64,2,2,64]{4,3,2,1,0:T(2,128)} reshape(f32[32,16384]{1,0:T(8,128)S(1)} %reduce.6) | data formatting | bytes 4194304
  212.5 3.6 %bitcast_bitcast_fusion = f32[64,32,2,2,64]{0,2,3,4,1:T(2,128)S(1)} fusion(f32[32,64,2,2,64]{4,3,2,1,0:T(2,128)} %reshape.119), kind=kLoop, calls=%fused_computation.58 | loop fusion | bytes 4194304 | tf_op jit(solution)/shard_map/transpose | solution.py:60
  216.1 2.4 copy.128
  218.5 3.7 %fusion = f32[64,64]{1,0:T(8,128)S(1)} fusion(f32[64,64,2,64]{0,1,2,3:T(8,128)S(1)} %bitcast.112, f32[64,2,64,64]{2,0,1,3:T(8,128)S(1)} %copy-done.1), kind=kOutput, calls=%fused_computation.9 | convolution fusion | flops 402657280 | bytes 4210688 | tf_op jit(solution)/shard_map/prlk,tlpk->rt/dot_general | solution.py:111
  222.2 0.1 reshape.120
  222.3 15.7 %all_to_all.40 = f32[32,1,128]{2,1,0:T(1,128)S(1)} all-to-all(f32[32,1,128]{2,1,0:T(1,128)S(1)} %reshape.120), channel_id=1, replica_groups=mesh['seq'=8,'blk'=32] {'blk'}, dimensions={0} | all-to-all | bytes 32768 | tf_op jit(solution)/shard_map/all_to_all | solution.py:115
  238.0 0.7 reduce.7
  238.7 0.1 reshape.121
  238.8 0.7 all_to_all.34
  (34 shorter events, 0.7 us)
Async XLA Ops:
  0.0 1.2 copy-start
  0.0 5.7 %copy-start.3 = (bf16[2,64,4096]{2,1,0:T(8,128)(2,1)S(1)}, bf16[2,64,4096]{2,1,0:T(8,128)(2,1)}, u32[]{:S(2)}) copy-start(bf16[2,64,4096]{2,1,0:T(8,128)(2,1)} %param.12) | copy-start | bytes 3145732
  0.0 5.7 %copy-start.2 = (bf16[2,2,128,4096]{3,2,1,0:T(8,128)(2,1)S(1)}, bf16[2,2,128,4096]{3,2,1,0:T(8,128)(2,1)}, u32[]{:S(2)}) copy-start(bf16[2,2,128,4096]{3,2,1,0:T(8,128)(2,1)} %param.9) | copy-start | bytes 12582916
  5.4 9.4 %copy-start.4 = (s32[2]{0:T(128)S(1)}, s32[2]{0:T(128)}, u32[]{:S(2)}) copy-start(s32[2]{0:T(128)} %param.11) | copy-start | bytes 28
  8.8 11.5 %all-to-all-start = ((f32[8,8,2,256]{3,1,2,0:T(8,128)}), f32[8,8,2,256]{3,1,2,0:T(8,128)S(1)}, u32[]{:S(2)}, u32[]{:S(2)}) async-start(f32[8,8,2,256]{3,1,2,0:T(8,128)} %copy.111), calls=%async_computation | async-start | bytes 262144 | tf_op jit(solution)/shard_map/all_to_all | solution.py:17
  21.5 26.1 %all-to-all-start.1 = ((f32[32,1,2049]{2,1,0:T(1,128)}), f32[32,1,2049]{2,1,0:T(1,128)S(1)}, u32[]{:S(2)}, u32[]{:S(2)}) async-start(f32[32,1,2049]{2,1,0:T(1,128)} %broadcast_in_dim.37), calls=%async_computation.1 | async-start | bytes 557056 | tf_op jit(solution)/shard_map/all_to_all | solution.py:34
  117.6 8.5 %all-to-all-start.2 = ((f32[8,1,2048]{2,1,0:T(1,128)}), f32[8,1,2048]{2,1,0:T(1,128)S(1)}, u32[]{:S(2)}, u32[]{:S(2)}) async-start(f32[8,1,2048]{2,1,0:T(1,128)} %reshape.116), calls=%async_computation.2 | async-start | bytes 131072 | tf_op jit(solution)/shard_map/all_to_all | solution.py:34
  138.4 62.3 %all-to-all-start.3 = ((f32[32,1,16384]{2,1,0:T(1,128)}), f32[32,1,16384]{2,1,0:T(1,128)}, u32[]{:S(2)}, u32[]{:S(2)}) async-start(f32[32,1,16384]{2,1,0:T(1,128)} %reshape.118), calls=%async_computation.3 | async-start | bytes 4194304 | tf_op jit(solution)/shard_map/all_to_all | solution.py:34
  216.1 2.4 %copy-start.1 = (f32[64,2,64,64]{2,0,1,3:T(8,128)S(1)}, f32[64,2,64,64]{2,0,1,3:T(8,128)}, u32[]{:S(2)}) copy-start(f32[64,2,64,64]{2,0,1,3:T(8,128)} %copy.129) | copy-start | bytes 6291460
where the time goes:
time: 240 us; the launch traced here: 239 us
  waiting for transfers between devices  66.4 us (28%)
  other arithmetic  55.8 us (23%)
  blocking collectives  37.6 us (16%)
  starting transfers between devices  34.6 us (14%)
  local copies, waits for them, and re-layouts  32.5 us (14%)
  matrix products  11.6 us (5%)
    all_to_all x3, waiting for transfers between devices, sent_to_all(): return lax.all_to_all(copies, axis, split_axis=0, concat_axis=0, tiled=True)  62.1 us
    all_to_all x3, starting transfers between devices, sent_to_all(): return lax.all_to_all(copies, axis, split_axis=0, concat_axis=0, tiled=True)  28.6 us
    another operation x6, other arithmetic, damped_inverse(): factor_low = jnp.linalg.cholesky(damped)  23.7 us
    unnamed x21, local copies, waits for them, and re-layouts  22 us
    all_gather x1, blocking collectives, sent_together_2(): whole = lax.all_gather(both, axis, axis=dim, tiled=True)  21.9 us
    another operation x4, other arithmetic, damped_inverse(): jax.scipy.linalg.cho_solve((lower, True), identity)  19.8 us
    all_to_all x1, blocking collectives, shards(): lax.all_to_all(local_scores, 'blk', split_axis=0, concat_axis=1, tiled=True)  15.7 us
    all_to_all x2, other arithmetic, sent_to_all(): return lax.all_to_all(copies, axis, split_axis=0, concat_axis=0, tiled=True)  8.19 us
  transfers between devices with their start and end apart: 4, of which 4 were waited for; matrix products, arithmetic and copies ran while one was open for 3% of the time, Pallas kernels for 0%

commit v1 on v0

--- a/solution.py
+++ b/solution.py
@@ -112,7 +112,12 @@
         * norm_scale
     )
     local_scores = lax.dynamic_update_slice_in_dim(empty_scores, partial_scores, jnp.int32(0), 0)
-    return lax.all_to_all(local_scores, "blk", split_axis=0, concat_axis=1, tiled=True)
+    return jnp.concatenate(
+        lax.all_to_all(
+            jnp.stack(jnp.split(local_scores, lax.axis_size("blk"), axis=0)), "blk", 0, 0
+        ),
+        axis=1,
+    )
 
 
 def solution(mesh):

time: 240 us -> 241 us (level)
    unnamed x21 -> x52, local copies, waits for them, and re-layouts: 22 us -> 22.4 us
where the time goes in v1:
time: 241 us; the launch traced here: 240 us
  waiting for transfers between devices  66.4 us (28%)
  other arithmetic  55.8 us (23%)
  blocking collectives  37.6 us (16%)
  starting transfers between devices  34.6 us (14%)
  local copies, waits for them, and re-layouts  32.9 us (14%)
  matrix products  11.6 us (5%)
    all_to_all x3, waiting for transfers between devices, sent_to_all(): return lax.all_to_all(copies, axis, split_axis=0, concat_axis=0, tiled=True)  62.1 us
    all_to_all x3, starting transfers between devices, sent_to_all(): return lax.all_to_all(copies, axis, split_axis=0, concat_axis=0, tiled=True)  28.6 us
    another operation x6, other arithmetic, damped_inverse(): factor_low = jnp.linalg.cholesky(damped)  23.7 us
    unnamed x52, local copies, waits for them, and re-layouts  22.4 us
    all_gather x1, blocking collectives, sent_together_2(): whole = lax.all_gather(both, axis, axis=dim, tiled=True)  21.9 us
    another operation x4, other arithmetic, damped_inverse(): jax.scipy.linalg.cho_solve((lower, True), identity)  19.8 us
    all_to_all x1, blocking collectives, shards(): lax.all_to_all(jnp.stack(jnp.split(local_scores, lax.axis_size('blk'), ax...  15.7 us
    all_to_all x2, other arithmetic, sent_to_all(): return lax.all_to_all(copies, axis, split_axis=0, concat_axis=0, tiled=True)  8.19 us
  transfers between devices with their start and end apart: 4, of which 4 were waited for; matrix products, arithmetic and copies ran while one was open for 3% of the time, Pallas kernels for 0%

profile of v1, /device:TPU:1, one launch (start us, length us, event | category | flops | bytes accessed | tf_op | source)
XLA Modules:
  0.0 239.9 jit_solution(16061646483151694435)
XLA Ops:
  0.0 0.9 compare_convert_fusion
  0.9 0.3 copy-done
  1.2 4.1 %convolution_multiply_fusion = f32[2,2,128,64]{2,3,1,0:T(8,128)S(1)} fusion(bf16[2,2,128,4096]{3,2,1,0:T(8,128)(2,1)} %param.10, bf16[2,64,4096]{2,1,0:T(8,128)(2,1)S(1)} %copy-done, f32[2,128]{1,0:T(2,128)S(1)} %compare_convert_fusion), kind=kOutput, calls=%fused_computation.2 | convolution fusion | flops 268468224 | bytes 5374976 | tf_op jit(solution)/shard_map/lrsd,lkd->lrsk/dot_general | solution.py:92
  5.4 0.3 convolution_bitcast_fusion.4
  5.7 1.4 convolution_multiply_fusion.1
  7.1 0.3 convolution_bitcast_fusion.1
  7.4 0.3 convolution_bitcast_fusion.5
  7.9 0.1 copy.107
  8.0 0.1 concatenate.16
  8.1 0.1 pad_maximum_fusion
  8.2 0.6 copy.110
  8.8 5.9 %all-to-all-start = ((f32[8,8,2,256]{3,1,2,0:T(8,128)}), f32[8,8,2,256]{3,1,2,0:T(8,128)S(1)}, u32[]{:S(2)}, u32[]{:S(2)}) async-start(f32[8,8,2,256]{3,1,2,0:T(8,128)} %copy.110), calls=%async_computation | async-start | bytes 262144 | tf_op jit(solution)/shard_map/all_to_all | solution.py:17
  14.8 0.6 reduce_sum.44
  16.1 4.3 %all-to-all-done = f32[8,8,2,256]{3,1,2,0:T(8,128)S(1)} async-done(((f32[8,8,2,256]{3,1,2,0:T(8,128)}), f32[8,8,2,256]{3,1,2,0:T(8,128)S(1)}, u32[]{:S(2)}, u32[]{:S(2)}) %all-to-all-start) | async-done | bytes 131104 | tf_op jit(solution)/shard_map/all_to_all | solution.py:17
  20.4 0.1 reshape.103
  20.5 0.1 reshape.104
  20.6 0.8 broadcast_in_dim.37
  21.5 12.9 %all-to-all-start.1 = ((f32[32,1,2049]{2,1,0:T(1,128)}), f32[32,1,2049]{2,1,0:T(1,128)S(1)}, u32[]{:S(2)}, u32[]{:S(2)}) async-start(f32[32,1,2049]{2,1,0:T(1,128)} %broadcast_in_dim.37), calls=%async_computation.1 | async-start | bytes 557056 | tf_op jit(solution)/shard_map/all_to_all | solution.py:34
  34.5 0.1 reshape.109
  34.6 13.0 %all-to-all-done.1 = f32[32,1,2049]{2,1,0:T(1,128)S(1)} async-done(((f32[32,1,2049]{2,1,0:T(1,128)}), f32[32,1,2049]{2,1,0:T(1,128)S(1)}, u32[]{:S(2)}, u32[]{:S(2)}) %all-to-all-start.1) | async-done | bytes 262304 | tf_op jit(solution)/shard_map/all_to_all | solution.py:34
  47.6 0.2 reduce_sum.45
  47.7 0.5 slice.40
  48.2 0.1 reshape.106
  48.4 21.9 %all_gather.3 = f32[64,4,64]{2,1,0:T(4,128)S(1)} all-gather(f32[8,4,64]{2,1,0:T(4,128)S(1)} %pad_maximum_fusion.1), channel_id=1, replica_groups=mesh['seq'=8,'blk'=32] {'seq'}, dimensions={0}, use_global_device_ids=true | all-gather | bytes 73728 | tf_op jit(solution)/shard_map/all_gather | solution.py:53
  70.4 0.1 copy.146
  70.5 0.1 copy.144
  70.6 0.8 fusion.15
  71.4 0.7 bitcast_add_fusion.3
  72.2 11.7 %custom-call.10 = f32[2,64,64]{2,1,0:T(8,128)S(1)} custom-call(f32[2,64,64]{2,1,0:T(8,128)S(1)} %fusion.14), custom_call_target="Cholesky" | custom-call | tf_op jit(solution)/shard_map/jit(cholesky)/cholesky | solution.py:74
  83.9 0.1 copy.122
  84.0 11.7 %custom-call.12 = f32[2,64,64]{2,1,0:T(8,128)S(1)} custom-call(f32[2,64,64]{2,1,0:T(8,128)S(1)} %fusion.9), custom_call_target="Cholesky" | custom-call | tf_op jit(solution)/shard_map/jit(cholesky)/cholesky | solution.py:74
  95.8 0.1 compare_reduce_fusion.1
  95.9 0.1 compare_reduce_fusion
  96.1 0.1 select_bitcast_fusion.1
  96.2 9.8 %custom-call.11 = f32[2,1,64,64]{2,3,1,0:T(8,128)S(1)} custom-call(f32[2,1,64,64]{3,2,1,0:T(8,128)S(1)} %get-tuple-element.19), custom_call_target="InvertDiagBlocksLowerTriangular" | custom-call | tf_op jit(solution)/shard_map/vmap(jit(_cho_solve))/triangular_solve | solution.py:75
  106.0 9.8 %custom-call.13 = f32[2,1,64,64]{2,3,1,0:T(8,128)S(1)} custom-call(f32[2,1,64,64]{3,2,1,0:T(8,128)S(1)} %get-tuple-element.20), custom_call_target="InvertDiagBlocksLowerTriangular" | custom-call | tf_op jit(solution)/shard_map/vmap(jit(_cho_solve))/triangular_solve | solution.py:75
  115.8 0.3 fusion.7
  116.1 0.3 fusion.12
  116.4 0.2 convolution_bitcast_fusion.3
  116.6 0.2 convolution_bitcast_fusion.7
  116.8 0.7 reshape.121
  117.6 3.5 %all-to-all-start.2 = ((f32[8,1,2048]{2,1,0:T(1,128)}), f32[8,1,2048]{2,1,0:T(1,128)S(1)}, u32[]{:S(2)}, u32[]{:S(2)}) async-start(f32[8,1,2048]{2,1,0:T(1,128)} %reshape.121), calls=%async_computation.2 | async-start | bytes 131072 | tf_op jit(solution)/shard_map/all_to_all | solution.py:34
  121.1 0.2 convolution_bitcast_fusion.2
  121.3 4.7 %all-to-all-done.2 = f32[8,1,2048]{2,1,0:T(1,128)S(1)} async-done(((f32[8,1,2048]{2,1,0:T(1,128)}), f32[8,1,2048]{2,1,0:T(1,128)S(1)}, u32[]{:S(2)}, u32[]{:S(2)}) %all-to-all-start.2) | async-done | bytes 65568 | tf_op jit(solution)/shard_map/all_to_all | solution.py:34
  126.1 0.5 broadcast.96
  126.6 0.8 reduce.5
  127.4 0.1 reshape.122
  127.5 0.4 convolution_bitcast_fusion
  127.8 0.1 copy.126
  128.0 3.8 %broadcast_bitcast_fusion = f32[32,64,2,2,64]{4,3,2,1,0:T(2,128)} fusion(f32[64,2,2,64]{0,1,2,3:T(2,128)S(1)} %copy.126), kind=kLoop, calls=%fused_computation.123 | loop fusion | bytes 2162688
  131.8 6.6 %reshape.123 = f32[32,1,16384]{2,1,0:T(1,128)} reshape(f32[32,64,2,2,64]{4,3,2,1,0:T(2,128)} %broadcast_bitcast_fusion) | data formatting | bytes 4194304
  138.4 12.3 %all-to-all-start.3 = ((f32[32,1,16384]{2,1,0:T(1,128)}), f32[32,1,16384]{2,1,0:T(1,128)}, u32[]{:S(2)}, u32[]{:S(2)}) async-start(f32[32,1,16384]{2,1,0:T(1,128)} %reshape.123), calls=%async_computation.3 | async-start | bytes 4194304 | tf_op jit(solution)/shard_map/all_to_all | solution.py:34
  150.6 5.7 %copy.128 = f32[64,2,64,64]{2,0,1,3:T(8,128)} copy(f32[64,2,64,64]{3,2,1,0:T(8,128)} %param.14) | data formatting | bytes 4194304 | tf_op args[5]
  156.3 44.4 %all-to-all-done.3 = f32[32,1,16384]{2,1,0:T(1,128)} async-done(((f32[32,1,16384]{2,1,0:T(1,128)}), f32[32,1,16384]{2,1,0:T(1,128)}, u32[]{:S(2)}, u32[]{:S(2)}) %all-to-all-start.3) | async-done | bytes 2097184 | tf_op jit(solution)/shard_map/all_to_all | solution.py:34
  200.7 7.4 %reduce.6 = f32[32,16384]{1,0:T(8,128)S(1)} reduce(f32[32,1,16384]{2,1,0:T(1,128)} %all-to-all-done.3, f32[]{:T(128)} %broadcast.96), dimensions={1}, to_apply=%all_to_all.19.reduce_sub_computation | reduce | bytes 4194308 | tf_op jit(solution)/shard_map/all_to_all | solution.py:34
  208.1 4.4 %reshape.124 = f32[32,64,2,2,64]{4,3,2,1,0:T(2,128)} reshape(f32[32,16384]{1,0:T(8,128)S(1)} %reduce.6) | data formatting | bytes 4194304
  212.5 3.6 %bitcast_bitcast_fusion = f32[64,32,2,2,64]{0,2,3,4,1:T(2,128)S(1)} fusion(f32[32,64,2,2,64]{4,3,2,1,0:T(2,128)} %reshape.124), kind=kLoop, calls=%fused_computation.122 | loop fusion | bytes 4194304 | tf_op jit(solution)/shard_map/transpose | solution.py:60
  216.1 2.4 copy.127
  218.5 3.7 %fusion = f32[64,64]{1,0:T(8,128)S(1)} fusion(f32[64,64,2,64]{0,1,2,3:T(8,128)S(1)} %bitcast.239, f32[64,2,64,64]{2,0,1,3:T(8,128)S(1)} %copy-done.1), kind=kOutput, calls=%fused_computation.9 | convolution fusion | flops 402657280 | bytes 4210688 | tf_op jit(solution)/shard_map/prlk,tlpk->rt/dot_general | solution.py:111
  222.6 0.1 reshape.125
  222.7 15.7 %all_to_all.26 = f32[32,1,128]{2,1,0:T(1,128)S(1)} all-to-all(f32[32,1,128]{2,1,0:T(1,128)S(1)} %reshape.125), channel_id=1, replica_groups=mesh['seq'=8,'blk'=32] {'blk'}, dimensions={0} | all-to-all | bytes 32768 | tf_op jit(solution)/shard_map/all_to_all | solution.py:116
  238.4 0.7 reduce.7
  239.1 0.1 reshape.126
  239.2 0.7 reshape.113
  (66 shorter events, 1.0 us)
Async XLA Ops:
  0.0 1.2 copy-start
  0.0 5.7 %copy-start.3 = (bf16[2,64,4096]{2,1,0:T(8,128)(2,1)S(1)}, bf16[2,64,4096]{2,1,0:T(8,128)(2,1)}, u32[]{:S(2)}) copy-start(bf16[2,64,4096]{2,1,0:T(8,128)(2,1)} %param.12) | copy-start | bytes 3145732
  0.0 5.7 %copy-start.2 = (bf16[2,2,128,4096]{3,2,1,0:T(8,128)(2,1)S(1)}, bf16[2,2,128,4096]{3,2,1,0:T(8,128)(2,1)}, u32[]{:S(2)}) copy-start(bf16[2,2,128,4096]{3,2,1,0:T(8,128)(2,1)} %param.9) | copy-start | bytes 12582916
  5.4 9.4 %copy-start.4 = (s32[2]{0:T(128)S(1)}, s32[2]{0:T(128)}, u32[]{:S(2)}) copy-start(s32[2]{0:T(128)} %param.11) | copy-start | bytes 28
  8.8 11.5 %all-to-all-start = ((f32[8,8,2,256]{3,1,2,0:T(8,128)}), f32[8,8,2,256]{3,1,2,0:T(8,128)S(1)}, u32[]{:S(2)}, u32[]{:S(2)}) async-start(f32[8,8,2,256]{3,1,2,0:T(8,128)} %copy.110), calls=%async_computation | async-start | bytes 262144 | tf_op jit(solution)/shard_map/all_to_all | solution.py:17
  21.5 26.1 %all-to-all-start.1 = ((f32[32,1,2049]{2,1,0:T(1,128)}), f32[32,1,2049]{2,1,0:T(1,128)S(1)}, u32[]{:S(2)}, u32[]{:S(2)}) async-start(f32[32,1,2049]{2,1,0:T(1,128)} %broadcast_in_dim.37), calls=%async_computation.1 | async-start | bytes 557056 | tf_op jit(solution)/shard_map/all_to_all | solution.py:34
  117.6 8.5 %all-to-all-start.2 = ((f32[8,1,2048]{2,1,0:T(1,128)}), f32[8,1,2048]{2,1,0:T(1,128)S(1)}, u32[]{:S(2)}, u32[]{:S(2)}) async-start(f32[8,1,2048]{2,1,0:T(1,128)} %reshape.121), calls=%async_computation.2 | async-start | bytes 131072 | tf_op jit(solution)/shard_map/all_to_all | solution.py:34
  138.4 62.3 %all-to-all-start.3 = ((f32[32,1,16384]{2,1,0:T(1,128)}), f32[32,1,16384]{2,1,0:T(1,128)}, u32[]{:S(2)}, u32[]{:S(2)}) async-start(f32[32,1,16384]{2,1,0:T(1,128)} %reshape.123), calls=%async_computation.3 | async-start | bytes 4194304 | tf_op jit(solution)/shard_map/all_to_all | solution.py:34
  216.1 2.4 copy-start.1
